TPU v7x, 32 devices: a whole 2x2x4 slice. The times are simulated.
32 devices in a mesh: expert: 8 (over z, core), row: 4 (over y, x).
Axes of the slice: x: 2, y: 2, z: 4, core: 2. Of those that a mesh axis runs over, the one named last changes fastest.
Arguments:
- grads: bfloat16 [8, 7168, 2048], P('expert', 'row')
- basis: bfloat16 [8, 7168, 256], P('expert', 'row'), may hold values from -0.0625 to 0.0625
- loads: int32 [8], P('expert'), may hold values from 1 to 1, as said below
- flags: int32 [8], P('expert'), may hold values 0 or 1
Outputs:
- new_basis: float32 [8, 7168, 256], P('expert', 'row')
- rotated: float32 [8, 256, 2048], P('expert', None, 'row')
Inputs may be any that keep to these rules, and one draw needn't show every extreme that they name: Slots 0 to loads[d] - 1 of expert-axis index d are live and hold experts; the others are empty. Some index has all 1 slots live.
All inputs are finite; a program needn't handle non-finite values. No bound on the sum of `flags` on one device may be relied on, other than what follows from the above.
Results may differ from a plain program's by a relative error of at most 0.006.
Values sent between devices are 32-bit elements; how exact they have to be, the bound alone decides.
A program may use at most 64 MiB of HBM per device.

v0:
```python
import jax
import jax.numpy as jnp
from jax import lax
from jax.sharding import PartitionSpec as P

D = 7168
S = 2048


def on_device(grads, basis, loads, flags):
    slot_count = grads.shape[0]
    live_count = loads[0]
    live_mask = jnp.arange(slot_count, dtype=jnp.int32) < live_count
    refresh = jnp.logical_and(live_mask, flags == 1)
    live_cube = live_mask[:, None, None]
    refresh_cube = refresh[:, None, None]
    squares = jnp.sum(jnp.where(live_cube, jnp.square(grads.astype(jnp.float32)), 0.0))
    leader = (lax.axis_index("row") == 0).astype(jnp.float32)
    total_sq, total_live = lax.psum(
        (squares, leader * live_count.astype(jnp.float32)), ("expert", "row")
    )
    norm_scale = lax.rsqrt(total_sq / (total_live * D * S) + 1e-06)
    local_inner = jnp.einsum("cds,cdk->csk", grads, basis, preferred_element_type=jnp.float32)
    inner_sum = jnp.stack([lax.psum(local_inner[0], "row")])
    inner_gram = jnp.einsum("csk,csj->ckj", inner_sum, inner_sum, precision=lax.Precision.HIGHEST)
    inner_half = inner_sum.astype(jnp.bfloat16)
    power_rows = jnp.einsum(
        "cds,csk->cdk", grads, inner_half, preferred_element_type=jnp.float32
    ).astype(jnp.bfloat16)
    projector = jnp.where(refresh_cube, power_rows, basis)
    local_cross = jnp.einsum("cdk,cds->cks", projector, grads, preferred_element_type=jnp.float32)
    identity = jnp.eye(basis.shape[2], dtype=jnp.float32)
    lower_first = jnp.linalg.cholesky(jnp.where(refresh_cube, inner_gram, identity))
    first_rows = lax.linalg.triangular_solve(
        lower_first, power_rows.astype(jnp.float32), left_side=False, lower=True, transpose_a=True
    )
    local_second = jnp.einsum(
        "cdk,cdj->ckj", first_rows, first_rows, precision=lax.Precision.HIGHEST
    )
    gram_again = lax.psum(local_second, "row")
    cross_cols = lax.psum_scatter(local_cross, "row", scatter_dimension=2, tiled=True)
    lower_second = jnp.linalg.cholesky(jnp.where(refresh_cube, gram_again, identity))
    fresh_basis = lax.linalg.triangular_solve(
        lower_second, first_rows, left_side=False, lower=True, transpose_a=True
    )
    half_solved = lax.linalg.triangular_solve(lower_first, cross_cols, left_side=True, lower=True)
    fresh_rot = lax.linalg.triangular_solve(lower_second, half_solved, left_side=True, lower=True)
    new_basis = jnp.where(
        refresh_cube, fresh_basis, jnp.where(live_cube, basis.astype(jnp.float32), 0.0)
    )
    rotated = jnp.where(refresh_cube, fresh_rot, jnp.where(live_cube, cross_cols, 0.0)) * norm_scale
    return (new_basis, rotated)


def solution(mesh):
    placed = (P("expert", "row", None), P("expert", "row", None), P("expert"), P("expert"))
    return jax.shard_map(
        on_device,
        mesh=mesh,
        in_specs=placed,
        out_specs=(P("expert", "row", None), P("expert", None, "row")),
        check_vma=False,
    )
```

profile of v0, /device:TPU:0, one launch (start us, length us, event | category | flops | bytes accessed | tf_op | source)
XLA Modules:
  0.0 307.6 jit_solution(6141670956639925859)
XLA Ops:
  7.2 6.8 %fusion.4 = f32[2048,256]{1,0:T(8,128)} fusion(bf16[1,1792,2048]{2,1,0:T(8,128)(2,1)} %param.9, bf16[1,1792,256]{2,1,0:T(8,128)(2,1)} %param.10), kind=kOutput, calls=%fused_computation.9 | convolution fusion | flops 1879048192 | bytes 10354688 | tf_op jit(solution)/shard_map/cds,cdk->csk/dot_general | solution.py:23
  14.1 1.1 copy-done.2
  15.2 1.1 copy.12
  17.7 68.7 %all-reduce.5.cloned.1.call-done = f32[2048,256]{1,0:T(8,128)} async-done(((f32[2048,256]{1,0:T(8,128)}), f32[2048,256]{1,0:T(8,128)}) %all-reduce.5.cloned.1.call-update) | async-done | bytes 2097168 | tf_op jit(solution)/shard_map/psum | solution.py:24
  86.4 5.7 %convolution_select_fusion = f32[256,256]{0,1:T(8,128)S(1)} fusion(f32[2048,256]{1,0:T(8,128)} %all-reduce.5.cloned.1.call-done, pred[]{:T(512)} %bitcast), kind=kOutput, calls=%fused_computation.32 | convolution fusion | flops 1610809344 | bytes 2359297 | tf_op jit(solution)/shard_map/csk,csj->ckj/dot_general | solution.py:25
  93.0 11.7 %custom-call.21 = f32[1,128,128]{2,1,0:T(8,128)S(1)} custom-call(f32[1,128,128]{2,1,0:T(8,128)S(1)} %cholesky.191), custom_call_target="Cholesky" | custom-call | tf_op jit(solution)/shard_map/jit(cholesky)/cholesky | solution.py:33
  104.7 9.8 %custom-call.22 = f32[1,1,128,128]{2,3,1,0:T(8,128)S(1)} custom-call(f32[1,1,128,128]{3,2,1,0:T(8,128)S(1)} %get-tuple-element.68), custom_call_target="InvertDiagBlocksLowerTriangular" | custom-call | tf_op jit(solution)/shard_map/jit(cholesky)/cholesky | solution.py:33
  114.6 1.0 bitcast_dynamic-update-slice_fusion.3
  115.6 1.1 fusion.27
  116.7 11.9 %custom-call.23 = f32[1,128,128]{2,1,0:T(8,128)S(1)} custom-call(f32[1,128,128]{2,1,0:T(8,128)S(1)} %fusion.27), custom_call_target="Cholesky" | custom-call | tf_op jit(solution)/shard_map/jit(cholesky)/cholesky | solution.py:33
  130.7 3.9 %while.8 = (s32[]{:T(128)}, f32[1,256,256]{2,1,0:T(8,128)S(1)}, s32[2,2]{1,0:T(2,128)S(1)}, f32[2,1,128,128]{3,2,1,0:T(8,128)S(1)}, s32[]{:T(128)}) while((s32[]{:T(128)}, f32[1,256,256]{2,1,0:T(8,128)S(1)}, s32[2,2]{1,0:T(2,128)S(1)}, f32[2,1,128,128]{3,2,1,0:T(8,128)S(1)}, s32[]{:T(128)}) %tuple.57), condition=%wide.while_cond, body=%wide.while_body.sunk | while | flops 2 | bytes 131181 | solution.py:34
  131.3 1.4 bitcast_dynamic-update-slice_fusion.6
  133.3 1.4 bitcast_dynamic-update-slice_fusion.6
  134.6 19.7 %custom-call.24 = f32[1,2,128,128]{2,3,1,0:T(8,128)S(1)} custom-call(f32[1,2,128,128]{3,2,1,0:T(8,128)S(1)} %bitcast.221), custom_call_target="InvertDiagBlocksLowerTriangular" | custom-call | tf_op jit(solution)/shard_map/triangular_solve/custom-call.0 | solution.py:34
  154.3 6.2 %fusion.53 = (f32[1,1792,256]{1,2,0:T(8,128)S(1)}, bf16[1,1792,256]{1,2,0:T(8,128)(2,1)}) fusion(bf16[1,1792,2048]{2,1,0:T(8,128)(2,1)} %param.9, f32[2048,256]{1,0:T(8,128)S(1)} %copy-done), kind=kOutput, calls=%fused_computation.99 | convolution fusion | flops 1880489984 | bytes 12189696 | tf_op jit(solution)/shard_map/cds,csk->cdk/dot_general | solution.py:27
  163.4 2.4 fusion.22
  165.9 6.8 %fusion.6 = f32[1,256,2048]{2,1,0:T(8,128)} fusion(bf16[1,1792,2048]{2,1,0:T(8,128)(2,1)} %param.9, bf16[1,1792,256]{1,2,0:T(8,128)(2,1)} %get-tuple-element.70, bf16[1,1792,256]{1,2,0:T(8,128)(2,1)S(1)} %copy.12, pred[]{:T(512)} %bitcast), kind=kOutput, calls=%fused_computation.11 | convolution fusion | flops 1879506944 | bytes 11272193 | tf_op jit(solution)/shard_map/cdk,cds->cks/dot_general | solution.py:31
  172.7 7.5 %select_reduce_fusion = f32[]{:T(128)} fusion(bf16[1,1792,2048]{2,1,0:T(8,128)(2,1)} %param.9, pred[]{:T(512)} %bitcast.40), kind=kLoop, calls=%fused_computation.4 | loop fusion | flops 14680063 | bytes 7340037 | tf_op jit(solution)/shard_map/reduce_sum | solution.py:17
  180.2 39.8 %all-reduce.1 = (f32[]{:T(128)}, f32[]{:T(128)}) all-reduce(f32[]{:T(128)} %select_reduce_fusion, f32[]{:T(128)S(6)} %mul.13), channel_id=1, replica_groups=mesh['expert'=8,'row'=4] {'expert','row'}, use_global_device_ids=true, to_apply=%region_8.12 | all-reduce | flops 2 | bytes 16 | tf_op jit(solution)/shard_map/psum | solution.py:19
  222.4 1.0 fusion.40
  223.4 12.3 %custom-call.25 = f32[1,128,128]{2,1,0:T(8,128)} custom-call(f32[1,128,128]{2,1,0:T(8,128)S(1)} %cholesky.194), custom_call_target="Cholesky" | custom-call | tf_op jit(solution)/shard_map/jit(cholesky)/cholesky | solution.py:42
  236.7 1.5 select_reduce_fusion.2
  238.1 11.3 %custom-call.26 = f32[1,1,128,128]{2,3,1,0:T(8,128)} custom-call(f32[1,1,128,128]{3,2,1,0:T(8,128)} %get-tuple-element.64), custom_call_target="InvertDiagBlocksLowerTriangular" | custom-call | tf_op jit(solution)/shard_map/jit(cholesky)/cholesky | solution.py:42
  249.4 1.0 bitcast_dynamic-update-slice_fusion.2
  251.4 12.5 %custom-call.27 = f32[1,128,128]{2,1,0:T(8,128)S(1)} custom-call(f32[1,128,128]{2,1,0:T(8,128)} %fusion.28), custom_call_target="Cholesky" | custom-call | tf_op jit(solution)/shard_map/jit(cholesky)/cholesky | solution.py:42
  266.6 4.0 %while.9 = (s32[]{:T(128)}, f32[1,256,256]{2,1,0:T(8,128)S(1)}, s32[2,2]{1,0:T(2,128)S(1)}, f32[2,1,128,128]{3,2,1,0:T(8,128)S(1)}, s32[]{:T(128)}) while((s32[]{:T(128)}, f32[1,256,256]{2,1,0:T(8,128)S(1)}, s32[2,2]{1,0:T(2,128)S(1)}, f32[2,1,128,128]{3,2,1,0:T(8,128)S(1)}, s32[]{:T(128)}) %tuple.69), condition=%wide.while_cond.clone, body=%wide.while_body.clone.sunk | while | flops 2 | bytes 131181 | solution.py:43
  267.2 1.4 bitcast_dynamic-update-slice_fusion.7
  269.2 1.4 bitcast_dynamic-update-slice_fusion.7
  270.6 19.9 %custom-call.28 = f32[1,2,128,128]{2,3,1,0:T(8,128)S(1)} custom-call(f32[1,2,128,128]{3,2,1,0:T(8,128)S(1)} %bitcast.220), custom_call_target="InvertDiagBlocksLowerTriangular" | custom-call | tf_op jit(solution)/shard_map/triangular_solve/custom-call.0 | solution.py:43
  293.6 1.7 copy.14
  295.3 1.4 fusion.38
  297.6 1.3 fusion.24
  (60 shorter events, 17.0 us)
Async XLA Ops:
  7.2 79.2 %all-reduce.5.cloned.1.call-start = ((), (), s32[]{:S(2)}) async-start(), calls=%async_computation.1 | async-start | bytes 4194304 | tf_op jit(solution)/shard_map/psum | solution.py:24
  14.0 1.2 copy-start.2
  14.1 207.2 %all-reduce.7.cloned.1.call-start = ((), (), s32[]{:S(2)}) async-start(), calls=%async_computation.2 | async-start | bytes 524288 | tf_op jit(solution)/shard_map/psum | solution.py:40
  92.1 62.3 %copy-start = (f32[2048,256]{1,0:T(8,128)S(1)}, f32[2048,256]{1,0:T(8,128)}, u32[]{:S(2)}) copy-start(f32[2048,256]{1,0:T(8,128)} %all-reduce.5.cloned.1.call-done) | copy-start | bytes 6291460
  92.3 0.7 copy-start.3
  154.3 8.1 %copy-start.4 = (f32[1,2,128,128]{2,3,1,0:T(8,128)}, f32[1,2,128,128]{2,3,1,0:T(8,128)S(1)}, u32[]{:S(2)}) copy-start(f32[1,2,128,128]{2,3,1,0:T(8,128)S(1)} %custom-call.24) | copy-start | bytes 393220
  165.8 129.5 %reduce-scatter.2.cloned.1.call-start = ((), (), s32[]{:S(2)}) async-start(), calls=%async_computation.3 | async-start | bytes 2621440 | tf_op jit(solution)/shard_map/reduce_scatter | solution.py:41
  293.6 1.7 copy-start.5
  295.3 4.4 %copy-start.1 = (f32[1,256,512]{2,1,0:T(8,128)S(1)}, f32[1,256,512]{2,1,0:T(8,128)}, u32[]{:S(2)}) copy-start(f32[1,256,512]{2,1,0:T(8,128)} %reduce-scatter.2.cloned.1.call-done) | copy-start | bytes 1572868
Sparse Core Ops, SparseCore 0:
  14.2 72.1 all-reduce.4
  165.9 43.0 all-reduce.6
  211.9 35.3 reduce-scatter.1
where the time goes:
time: 311 us; the launch traced here: 308 us
  other arithmetic  123 us (40%)
  waiting for transfers between devices  68.8 us (22%)
  matrix products  42 us (14%)
  blocking collectives  39.8 us (13%)
  between operations  19.7 us (6%)
  local copies, waits for them, and re-layouts  13.7 us (4%)
    psum x1, waiting for transfers between devices, on_device(): inner_sum = jnp.stack([lax.psum(local_inner[0], 'row')])  68.7 us
    psum x1, blocking collectives, on_device(): lax.psum((squares, leader * live_count.astype(jnp.float32)), ('expert', '...  39.8 us
    another operation x7, other arithmetic, on_device(): jnp.linalg.cholesky(jnp.where(refresh_cube, gram_again, identity))  39 us
    another operation x6, other arithmetic, on_device(): jnp.linalg.cholesky(jnp.where(refresh_cube, inner_gram, identity))  34.1 us
    another operation x2, other arithmetic, on_device(): lax.linalg.triangular_solve(lower_second, first_rows, left_side=False, lo...  20 us
    another operation x3, other arithmetic, on_device(): lax.linalg.triangular_solve(lower_first, power_rows.astype(jnp.float32),...  19.7 us
    reduce_sum x1, other arithmetic, on_device(): jnp.sum(jnp.where(live_cube, jnp.square(grads.astype(jnp.float32)), 0.0))  7.48 us
    dot_general x1, matrix products, on_device(): jnp.einsum('cds,cdk->csk', grads, basis, preferred_element_type=jnp.float32)  6.82 us
  transfers between devices with their start and end apart: 3, of which 1 were waited for; matrix products, arithmetic and copies ran while one was open for 29% of the time, Pallas kernels for 0%

commit v1 on v0

v1 whole, which is shorter than its diff:
```python
import functools

import jax
import jax.numpy as jnp
from jax import lax
from jax.experimental import pallas as pl
from jax.experimental.pallas import tpu as pltpu
from jax.sharding import PartitionSpec as P

PANEL = 16
HIGHEST = lax.Precision.HIGHEST
F32 = jnp.float32
BF16 = jnp.bfloat16


def dot(a, b, precision=None):
    return lax.dot_general(a, b, (((1,), (0,)), ((), ())), precision=precision, preferred_element_type=F32)


def dot_t(a, b, precision=None):
    return lax.dot_general(a, b, (((1,), (1,)), ((), ())), precision=precision, preferred_element_type=F32)


def first_bit(mask, order):
    for phase, bit in enumerate(order):
        if mask >> bit & 1:
            return phase
    return len(order)


def panel_step(work, step):
    size = work.shape[0]
    panel = work[0:PANEL, :]
    rows = lax.broadcasted_iota(jnp.int32, (PANEL, 128), 0)
    lanes = lax.broadcasted_iota(jnp.int32, (PANEL, 128), 1)
    columns = [jnp.broadcast_to(panel[:, j : j + 1], (PANEL, 128)) for j in range(PANEL)]
    pieces = [panel[:, at : at + 128] for at in range(0, size, 128)]
    unit = (rows == lanes).astype(F32)
    root = jnp.zeros((PANEL, 128), F32)
    for j in range(PANEL):
        inverse_root = lax.rsqrt(columns[j][j : j + 1, :])
        root = jnp.where(rows == j, inverse_root, root)
        factor = jnp.where(rows > j, columns[j] * (inverse_root * inverse_root), 0.0)
        for k in range(j + 1, PANEL):
            columns[k] = columns[k] - factor * columns[k][j : j + 1, :]
        pieces = [piece - factor * piece[j : j + 1, :] for piece in pieces]
        unit = unit - factor * unit[j : j + 1, :]
    scaled = [root * piece for piece in pieces]
    full = jnp.concatenate([jnp.where(lanes < PANEL, root * unit, scaled[0])] + scaled[1:], axis=1)
    where = lax.broadcasted_iota(jnp.int32, (PANEL, size), 1)
    open_columns = jnp.logical_and(where >= PANEL, where < size - PANEL * step)
    left = jnp.where(open_columns, jnp.concatenate(scaled, axis=1), 0.0)
    update = dot(left.T, full, HIGHEST)
    body = work[PANEL:, :]
    ahead = lax.broadcasted_iota(jnp.int32, body.shape, 1) < PANEL
    rest = jnp.where(ahead, 0.0, body) - update[PANEL:, :]
    work[0 : size - PANEL, :] = pltpu.roll(rest, size - PANEL, 1)
    work[size - PANEL :, :] = pltpu.roll(full, size - PANEL, 1)


def panel_steps(work, begin, end):
    def body(step, carry):
        panel_step(work, step)
        return carry

    lax.fori_loop(begin, end, body, 0)


def lower_of(work):
    shape = work.shape
    below = lax.broadcasted_iota(jnp.int32, shape, 1) <= lax.broadcasted_iota(jnp.int32, shape, 0)
    return jnp.where(below, work[...], 0.0)


def kernel(
    n, experts, entries, g_ref, b_ref, live_ref, refresh_ref, fresh_ref, rot_ref,
    bt, part, land, part2, land2, full, inner, power, power_t, first, work, inv1,
    gram, gram_land, total, total_land,
    s_rs, r_rs, s_ag, r_ag, s_rs2, r_rs2, s_gr, r_gr, s_tot, r_tot,
):
    bits = n.bit_length() - 1
    expert_bits = experts.bit_length() - 1
    depth, wide = g_ref.shape
    size = b_ref.shape[1]
    half = size // 2
    block = wide // n
    me = lax.axis_index("row")
    my_expert = lax.axis_index("expert")
    orders = [tuple(range(bits)), tuple(reversed(range(bits)))]

    def other(index, mask):
        at = index
        for bit in range(max(bits, expert_bits)):
            if mask >> bit & 1:
                at = at + (1 - 2 * (lax.rem(index // (1 << bit), 2))) * (1 << bit)
        return at

    def partner(bit):
        return {"row": other(me, 1 << bit), "expert": my_expert}

    def expert_partner(bit):
        return {"row": me, "expert": other(my_expert, 1 << bit)}

    everyone = [partner(b) for b in range(bits)] + [expert_partner(b) for b in range(expert_bits)]
    barrier = pltpu.get_barrier_semaphore()
    for peer in everyone:
        pl.semaphore_signal(barrier, inc=1, device_id=peer, device_id_type=pl.DeviceIdType.MESH)

    def columns(mask):
        return pl.ds(pl.multiple_of(other(me, mask) * block, block), block)

    def copy(src, dst, send, recv, to):
        return pltpu.make_async_remote_copy(
            src_ref=src, dst_ref=dst, send_sem=send, recv_sem=recv,
            device_id=to, device_id_type=pl.DeviceIdType.MESH,
        )

    moves = []
    for phase in range(bits):
        for h in range(2):
            order = orders[h]
            masks = [m for m in range(n) if first_bit(m, order) == phase]
            masks.sort(key=lambda m: first_bit(m & ~(1 << order[phase]), order))
            moves.append([(h, phase, m, m & ~(1 << order[phase])) for m in masks])
    schedule = []
    for phase in range(bits):
        a, b = moves[2 * phase], moves[2 * phase + 1]
        schedule.append([move for pair in zip(a, b) for move in pair])
    slot = {}
    for phase_moves in schedule:
        for h, phase, m, there in phase_moves:
            slot[h, phase, there] = len(slot)

    def halving(part_ref, land_ref, sends, recvs):
        def make(h, phase, m, there):
            at = slot[h, phase, there]
            return copy(part_ref.at[h, m], land_ref.at[at], sends.at[at], recvs.at[at], partner(orders[h][phase]))

        def absorb(h, phase, m):
            at = slot[h, phase, m]
            back = m | 1 << orders[h][phase]
            make(h, phase, back, m).wait_recv()
            part_ref[h, m] = part_ref[h, m] + land_ref[at]

        return make, absorb

    def begin(left_ref, part_ref, make):
        started = set()
        for move in schedule[0]:
            h, _, m, _ = move
            part_ref[h, m] = dot(left_ref[h * half : (h + 1) * half, :], g_ref[:, columns(m)])
            make(*move).start()
            started.add((h, m))
        for m in range(n):
            for h in range(2):
                if (h, m) not in started:
                    part_ref[h, m] = dot(left_ref[h * half : (h + 1) * half, :], g_ref[:, columns(m)])

    def forward(make, absorb):
        for phase in range(1, bits):
            for move in schedule[phase]:
                h, _, m, _ = move
                for earlier in range(phase):
                    absorb(h, earlier, m)
                make(*move).start()

    def finish(make, absorb):
        for phase in range(bits):
            for h in range(2):
                absorb(h, phase, 0)
        for phase_moves in schedule:
            for move in phase_moves:
                make(*move).wait_send()

    def gram_exchange(use, between=None):
        for phase in range(bits):
            made = []
            for h in range(2):
                rows = slice(h * half, (h + 1) * half)
                made.append(copy(
                    gram.at[use, phase, rows], gram_land.at[use, phase, rows],
                    s_gr.at[use, phase, h], r_gr.at[use, phase, h], partner(orders[h][phase]),
                ))
            for item in made:
                item.start()
            if between is not None and phase == 0:
                between()
            for h, item in enumerate(made):
                rows = slice(h * half, (h + 1) * half)
                item.wait_recv()
                gram[use, phase + 1, rows] = gram[use, phase, rows] + gram_land[use, phase, rows]
            for item in made:
                item.wait_send()

    peers = everyone

    def total_copy(at):
        return copy(total.at[at], total_land.at[at], s_tot.at[at], r_tot.at[at], peers[at])

    def total_next(at):
        total_copy(at).wait()
        total[at + 1] = total[at] + total_land[at]
        if at + 1 < len(peers):
            total_copy(at + 1).start()

    live = live_ref[0] >= 1
    refresh = refresh_ref[0] == 1

    strip = 128 if depth % 128 == 0 else depth
    for at in range(0, depth, strip):
        bt[:, at : at + strip] = b_ref[at : at + strip, :].T

    pl.semaphore_wait(barrier, len(everyone))

    make, absorb = halving(part, land, s_rs, r_rs)
    begin(bt, part, make)

    def squares_of(step, sums):
        rows = g_ref[pl.ds(pl.multiple_of(step * 16, 16), 16), :].astype(F32)
        square = rows * rows
        for at in range(0, wide, 128):
            sums = sums + square[0:8, at : at + 128] + square[8:16, at : at + 128]
        return sums

    sums = lax.fori_loop(0, depth // 16, squares_of, jnp.zeros((8, 128), F32))
    total_sq = jnp.where(live, jnp.sum(sums), 0.0)
    count = jnp.where(jnp.logical_and(live, me == 0), 1.0, 0.0)
    tile_row = lax.broadcasted_iota(jnp.int32, (8, 128), 0)
    total[0] = jnp.where(tile_row == 0, total_sq, jnp.where(tile_row == 1, count, 0.0))
    total_copy(0).start()

    forward(make, absorb)
    finish(make, absorb)

    mine = jnp.concatenate([part[0, 0], part[1, 0]], axis=0).astype(BF16)
    gram[0, 0] = dot_t(mine, mine)
    gram_exchange(0)

    spread = []
    for h in range(2):
        order = tuple(reversed(orders[h]))
        held = [0]
        for bit in order:
            for m in list(held):
                spread.append((h, bit, m))
                held.append(m | 1 << bit)
    number = {(h, m | 1 << bit): at for at, (h, bit, m) in enumerate(spread)}

    def spread_copy(h, bit, m):
        at = number[h, m | 1 << bit]
        src = part.at[h, 0] if m == 0 else full.at[h, m]
        return copy(src, full.at[h, m | 1 << bit], s_ag.at[at], r_ag.at[at], partner(bit))

    arrived = set()

    def take(h, m):
        if m == 0 or (h, m) in arrived:
            return
        arrived.add((h, m))
        bit = next(b for (hh, b, mm) in spread if hh == h and mm | 1 << b == m)
        spread_copy(h, bit, m & ~(1 << bit)).wait_recv()

    def keep(h, m):
        source = part[h, 0] if m == 0 else full[h, m]
        inner[columns(m), h * half : (h + 1) * half] = source.T.astype(BF16)

    rank = {0: [], 1: []}
    for h, bit, m in spread:
        if m == 0:
            rank[h].append((h, bit, m))
    for pair in zip(rank[0], rank[1]):
        for item in pair:
            spread_copy(*item).start()
    work[...] = gram[0, bits]
    panels = size // PANEL
    panel_steps(work, 0, panels // 2)
    total_next(0)
    for h, bit, m in sorted((s for s in spread if s[2]), key=lambda s: bin(s[2]).count("1")):
        take(h, m)
        spread_copy(h, bit, m).start()
    panel_steps(work, panels // 2, panels)
    inv1[...] = lower_of(work)
    keep(0, 0)
    keep(1, 0)
    for m in sorted(range(1, n), key=lambda v: bin(v).count("1")):
        for h in range(2):
            take(h, m)
            keep(h, m)
    for item in spread:
        spread_copy(*item).wait_send()
    if len(peers) > 1:
        total_next(1)

    tile = 256 if depth % 256 == 0 else 64

    def power_rows(at):
        rows = slice(at, at + tile)
        power[rows, :] = dot(g_ref[rows, :], inner[...]).astype(BF16)
        power_t[:, rows] = power[rows, :].T

    for at in range(0, depth, tile):
        power_rows(at)
    first_t = dot(inv1[...], power_t[...].astype(F32), HIGHEST)
    gram[1, 0] = dot_t(first_t, first_t, HIGHEST)

    make2, absorb2 = halving(part2, land2, s_rs2, r_rs2)

    def beside():
        first[...] = dot_t(power[...].astype(F32), inv1[...], HIGHEST)

    gram_exchange(1, beside)
    begin(power_t, part2, make2)
    for at in range(2, len(peers) - 1):
        total_next(at)
    work[...] = gram[1, bits]
    panel_steps(work, 0, panels // 2)
    forward(make2, absorb2)
    panel_steps(work, panels // 2, panels)
    inv2 = lower_of(work)
    fresh = dot_t(first[...], inv2, HIGHEST)
    fresh_ref[...] = jnp.where(refresh, fresh, jnp.where(live, b_ref[...].astype(F32), 0.0))
    both = dot(inv2, inv1[...], HIGHEST)
    if len(peers) > 2:
        total_next(len(peers) - 1)
    final = total[len(peers)]
    norm = lax.rsqrt(final[0:1, 0:1] / (final[1:2, 0:1] * entries) + 1e-6)
    finish(make2, absorb2)
    cross = jnp.concatenate([part2[0, 0], part2[1, 0]], axis=0)
    stale = jnp.concatenate([part[0, 0], part[1, 0]], axis=0)
    turned = dot(both, cross, HIGHEST)
    rot_ref[...] = jnp.where(refresh, turned, jnp.where(live, stale, 0.0)) * norm


def on_device(n, experts, grads, basis, loads, flags):
    _, depth, wide = grads.shape
    size = basis.shape[2]
    block = wide // n
    bits = n.bit_length() - 1
    peers = bits + experts.bit_length() - 1
    moves = 2 * (n - 1)
    live = loads
    refresh = jnp.where(loads >= 1, flags, 0)
    vmem = pl.BlockSpec(memory_space=pltpu.VMEM)
    smem = pl.BlockSpec(memory_space=pltpu.SMEM)
    chunk = (size // 2, block)
    dma = pltpu.SemaphoreType.DMA
    new_basis, rotated = pl.pallas_call(
        functools.partial(kernel, n, experts, float(depth * n * wide)),
        out_shape=(
            jax.ShapeDtypeStruct((depth, size), F32),
            jax.ShapeDtypeStruct((size, block), F32),
        ),
        in_specs=[vmem, vmem, smem, smem],
        out_specs=(vmem, vmem),
        scratch_shapes=[
            pltpu.VMEM((size, depth), BF16),
            pltpu.VMEM((2, n, *chunk), F32),
            pltpu.VMEM((moves, *chunk), F32),
            pltpu.VMEM((2, n, *chunk), F32),
            pltpu.VMEM((moves, *chunk), F32),
            pltpu.VMEM((2, n, *chunk), F32),
            pltpu.VMEM((wide, size), BF16),
            pltpu.VMEM((depth, size), BF16),
            pltpu.VMEM((size, depth), BF16),
            pltpu.VMEM((depth, size), F32),
            pltpu.VMEM((size, size), F32),
            pltpu.VMEM((size, size), F32),
            pltpu.VMEM((2, bits + 1, size, size), F32),
            pltpu.VMEM((2, bits, size, size), F32),
            pltpu.VMEM((peers + 1, 8, 128), F32),
            pltpu.VMEM((peers, 8, 128), F32),
            dma((moves,)), dma((moves,)), dma((moves,)), dma((moves,)), dma((moves,)), dma((moves,)),
            dma((2, bits, 2)), dma((2, bits, 2)), dma((peers,)), dma((peers,)),
        ],
        compiler_params=pltpu.CompilerParams(
            collective_id=0, has_side_effects=True, vmem_limit_bytes=58 * 1024 * 1024
        ),
    )(grads[0], basis[0], live, refresh)
    return new_basis[None], rotated[None]


def solution(mesh):
    placed = (P("expert", "row", None), P("expert", "row", None), P("expert"), P("expert"))
    return jax.shard_map(
        functools.partial(on_device, mesh.shape["row"], mesh.shape["expert"]),
        mesh=mesh,
        in_specs=placed,
        out_specs=(P("expert", "row", None), P("expert", None, "row")),
        check_vma=False,
    )
```

time: 311 us -> 98.3 us (0.32); the launches traced: 308 us -> 98.1 us
  other arithmetic: 123 us -> 0 us
  Pallas kernels: 0 us -> 92.5 us
  waiting for transfers between devices: 68.8 us -> 0 us
  matrix products: 42 us -> 0 us
  blocking collectives: 39.8 us -> 0 us
  between operations: 19.7 us -> 1.94 us
  local copies, waits for them, and re-layouts: 13.7 us -> 3.7 us
    another operation x18 -> x0, other arithmetic: 113 us -> none  [the longest x7 39 us: on_device(): jnp.linalg.cholesky(jnp.where(refresh_cube, gram_again, identity))]
    pallas_call x0 -> x1, Pallas kernels: none -> 92.5 us  [on_device(): pl.pallas_call(functools.partial(kernel, n, experts, float(depth * n * wi...]
    psum x2 -> x0, waiting for transfers between devices: 68.7 us -> none  [the longest x1 68.7 us: on_device(): inner_sum = jnp.stack([lax.psum(local_inner[0], 'row')])]
    psum x1 -> x0, blocking collectives: 39.8 us -> none  [on_device(): lax.psum((squares, leader * live_count.astype(jnp.float32)), ('expert', '...]
    dot_general x5 -> x0, matrix products: 27.8 us -> none  [the longest x1 6.82 us: on_device(): jnp.einsum('cds,cdk->csk', grads, basis, preferred_element_type=jnp.float32)]
    another operation x16 -> x0, matrix products: 14.2 us -> none  [the longest x3 3.18 us: on_device(): lax.linalg.triangular_solve(lower_first, cross_cols, left_side=True, lowe...]
    another operation x19 -> x0, local copies, waits for them, and re-layouts: 8.82 us -> none  [the longest x9 3.98 us: on_device(): lax.linalg.triangular_solve(lower_first, power_rows.astype(jnp.float32),...]
    reduce_sum x1 -> x0, other arithmetic: 7.48 us -> none  [on_device(): jnp.sum(jnp.where(live_cube, jnp.square(grads.astype(jnp.float32)), 0.0))]
  transfers between devices with their start and end apart: 3 -> 0, of which waited for: 1 -> 0; matrix products, arithmetic and copies ran while one was open for 29% -> 0% of each run, Pallas kernels for 0% -> 0%
where the time goes in v1:
time: 98.3 us; the launch traced here: 98.1 us
  Pallas kernels  92.5 us (94%)
  local copies, waits for them, and re-layouts  3.7 us (4%)
  between operations  1.94 us (2%)
    pallas_call x1, Pallas kernels, on_device(): pl.pallas_call(functools.partial(kernel, n, experts, float(depth * n * wi...  92.5 us
    unnamed x4, local copies, waits for them, and re-layouts  3.7 us

profile of v1, /device:TPU:0, one launch (start us, length us, event | category | flops | bytes accessed | tf_op | source)
XLA Modules:
  0.0 98.1 jit_solution(15349406747659623433)
XLA Ops:
  1.9 92.5 %shard_map.59 = (f32[1792,256]{1,0:T(8,128)}, f32[256,512]{1,0:T(8,128)}) custom-call(bf16[1792,2048]{1,0:T(8,128)(2,1)} %bitcast.4, bf16[1792,256]{1,0:T(8,128)(2,1)} %bitcast.6, s32[1]{0:T(128)S(6)} %copy.8.live_ref, s32[1]{0:T(128)S(6)} %select_n.4.refresh_ref), custom_call_target="tpu_custom_call" | custom-call | tf_op jit(solution)/shard_map/pallas_call | solution.py:347
  94.4 0.0 copy-start
  94.4 2.9 %copy.10 = f32[1,1792,256]{2,1,0:T(8,128)} copy(f32[1,1792,256]{2,1,0:T(8,128)} %bitcast.5) | data formatting | bytes 3670016
  97.3 0.0 copy-done
  97.3 0.8 copy.11
Async XLA Ops:
  94.4 2.9 %copy-start = (f32[256,512]{1,0:T(8,128)S(1)}, f32[256,512]{1,0:T(8,128)}, u32[]{:S(2)}) copy-start(f32[256,512]{1,0:T(8,128)} %get-tuple-element.5) | copy-start | bytes 1572868

commit v2 on v1

--- a/solution.py
+++ b/solution.py
@@ -19,6 +19,14 @@
 
 def dot_t(a, b, precision=None):
     return lax.dot_general(a, b, (((1,), (1,)), ((), ())), precision=precision, preferred_element_type=F32)
+
+
+def pieces_of(x, count):
+    pieces = []
+    for _ in range(count):
+        pieces.append(x.astype(BF16))
+        x = x - pieces[-1].astype(F32)
+    return pieces
 
 
 def first_bit(mask, order):
@@ -73,14 +81,14 @@
 
 
 def kernel(
-    n, experts, entries, g_ref, b_ref, live_ref, refresh_ref, fresh_ref, rot_ref,
-    bt, part, land, part2, land2, full, inner, power, power_t, first, work, inv1,
+    n, experts, entries, g_hbm, b_ref, live_ref, refresh_ref, fresh_ref, rot_ref,
+    g_ref, g_sem, bt, part, land, part2, land2, full, inner, power_t, rough, tops, lows, top_rows, low_rows, work, inv1,
     gram, gram_land, total, total_land,
     s_rs, r_rs, s_ag, r_ag, s_rs2, r_rs2, s_gr, r_gr, s_tot, r_tot,
 ):
+    depth, wide = g_ref.shape
     bits = n.bit_length() - 1
     expert_bits = experts.bit_length() - 1
-    depth, wide = g_ref.shape
     size = b_ref.shape[1]
     half = size // 2
     block = wide // n
@@ -108,6 +116,9 @@
 
     def columns(mask):
         return pl.ds(pl.multiple_of(other(me, mask) * block, block), block)
+
+    def load(mask):
+        return pltpu.make_async_copy(g_hbm.at[:, columns(mask)], g_ref.at[:, columns(mask)], g_sem.at[mask])
 
     def copy(src, dst, send, recv, to):
         return pltpu.make_async_remote_copy(
@@ -144,14 +155,16 @@
 
         return make, absorb
 
-    def begin(left_ref, part_ref, make):
+    def begin(left_ref, part_ref, make, ensure=lambda m: None):
         started = set()
         for move in schedule[0]:
             h, _, m, _ = move
+            ensure(m)
             part_ref[h, m] = dot(left_ref[h * half : (h + 1) * half, :], g_ref[:, columns(m)])
             make(*move).start()
             started.add((h, m))
         for m in range(n):
+            ensure(m)
             for h in range(2):
                 if (h, m) not in started:
                     part_ref[h, m] = dot(left_ref[h * half : (h + 1) * half, :], g_ref[:, columns(m)])
@@ -183,8 +196,8 @@
                 ))
             for item in made:
                 item.start()
-            if between is not None and phase == 0:
-                between()
+            if between is not None:
+                between(phase)
             for h, item in enumerate(made):
                 rows = slice(h * half, (h + 1) * half)
                 item.wait_recv()
@@ -203,6 +216,12 @@
         if at + 1 < len(peers):
             total_copy(at + 1).start()
 
+    make, absorb = halving(part, land, s_rs, r_rs)
+    wanted = [move[2] for move in schedule[0]] + list(range(n))
+    wanted = sorted(range(n), key=wanted.index)
+    for m in wanted:
+        load(m).start()
+
     live = live_ref[0] >= 1
     refresh = refresh_ref[0] == 1
 
@@ -212,8 +231,14 @@
 
     pl.semaphore_wait(barrier, len(everyone))
 
-    make, absorb = halving(part, land, s_rs, r_rs)
-    begin(bt, part, make)
+    loaded = []
+
+    def ensure(m):
+        if m not in loaded:
+            load(m).wait()
+            loaded.append(m)
+
+    begin(bt, part, make, ensure)
 
     def squares_of(step, sums):
         rows = g_ref[pl.ds(pl.multiple_of(step * 16, 16), 16), :].astype(F32)
@@ -280,36 +305,57 @@
         spread_copy(h, bit, m).start()
     panel_steps(work, panels // 2, panels)
     inv1[...] = lower_of(work)
-    keep(0, 0)
-    keep(1, 0)
-    for m in sorted(range(1, n), key=lambda v: bin(v).count("1")):
+    tile = 256 if depth % 256 == 0 else 64
+    masks = sorted(range(n), key=lambda v: bin(v).count("1"))
+    for m in masks:
         for h in range(2):
             take(h, m)
             keep(h, m)
+        if m == masks[-1]:
+            break
+        for at in range(0, depth, tile):
+            rows = slice(at, at + tile)
+            term = dot(g_ref[rows, columns(m)], inner[columns(m), :])
+            rough[rows, :] = term if m == 0 else rough[rows, :] + term
+    for at in range(0, depth, tile):
+        rows = slice(at, at + tile)
+        last = dot(g_ref[rows, columns(masks[-1])], inner[columns(masks[-1]), :])
+        power_t[:, rows] = (rough[rows, :] + last).astype(BF16).T
+    one, two, three = pieces_of(inv1[...], 3)
+    for at in range(0, depth, tile):
+        rows = slice(at, at + tile)
+        block_t = power_t[:, rows]
+        once = dot(three, block_t) + dot(two, block_t) + dot(one, block_t)
+        tops[:, rows], lows[:, rows] = pieces_of(once, 2)
+    crossed = dot_t(tops[...], lows[...])
+    gram[1, 0] = dot_t(tops[...], tops[...]) + (dot_t(lows[...], lows[...]) + (crossed + crossed.T))
     for item in spread:
         spread_copy(*item).wait_send()
     if len(peers) > 1:
         total_next(1)
 
-    tile = 256 if depth % 256 == 0 else 64
-
-    def power_rows(at):
-        rows = slice(at, at + tile)
-        power[rows, :] = dot(g_ref[rows, :], inner[...]).astype(BF16)
-        power_t[:, rows] = power[rows, :].T
-
-    for at in range(0, depth, tile):
-        power_rows(at)
-    first_t = dot(inv1[...], power_t[...].astype(F32), HIGHEST)
-    gram[1, 0] = dot_t(first_t, first_t, HIGHEST)
-
     make2, absorb2 = halving(part2, land2, s_rs2, r_rs2)
 
-    def beside():
-        first[...] = dot_t(power[...].astype(F32), inv1[...], HIGHEST)
+    def cross_part(h, m):
+        part2[h, m] = dot(power_t[h * half : (h + 1) * half, :], g_ref[:, columns(m)])
+
+    def beside(phase):
+        if phase == 0:
+            for h, _, m, _ in schedule[0]:
+                cross_part(h, m)
+        if phase == bits - 1:
+            for move in schedule[0]:
+                make2(*move).start()
+            started = [(move[0], move[2]) for move in schedule[0]]
+            for h, m in [(h, m) for m in range(n) for h in range(2)]:
+                if (h, m) not in started:
+                    cross_part(h, m)
+            for at in range(0, depth, tile):
+                rows = slice(at, at + tile)
+                top_rows[rows, :] = tops[:, rows].T
+                low_rows[rows, :] = lows[:, rows].T
 
     gram_exchange(1, beside)
-    begin(power_t, part2, make2)
     for at in range(2, len(peers) - 1):
         total_next(at)
     work[...] = gram[1, bits]
@@ -317,8 +363,11 @@
     forward(make2, absorb2)
     panel_steps(work, panels // 2, panels)
     inv2 = lower_of(work)
-    fresh = dot_t(first[...], inv2, HIGHEST)
-    fresh_ref[...] = jnp.where(refresh, fresh, jnp.where(live, b_ref[...].astype(F32), 0.0))
+    high, low = pieces_of(inv2.T, 2)
+    for at in range(0, depth, tile):
+        rows = slice(at, at + tile)
+        fresh = dot(low_rows[rows, :], high) + dot(top_rows[rows, :], low) + dot(top_rows[rows, :], high)
+        fresh_ref[rows, :] = jnp.where(refresh, fresh, jnp.where(live, b_ref[rows, :].astype(F32), 0.0))
     both = dot(inv2, inv1[...], HIGHEST)
     if len(peers) > 2:
         total_next(len(peers) - 1)
@@ -350,9 +399,11 @@
             jax.ShapeDtypeStruct((depth, size), F32),
             jax.ShapeDtypeStruct((size, block), F32),
         ),
-        in_specs=[vmem, vmem, smem, smem],
+        in_specs=[pl.BlockSpec(memory_space=pl.ANY), vmem, smem, smem],
         out_specs=(vmem, vmem),
         scratch_shapes=[
+            pltpu.VMEM((depth, wide), BF16),
+            pltpu.SemaphoreType.DMA((n,)),
             pltpu.VMEM((size, depth), BF16),
             pltpu.VMEM((2, n, *chunk), F32),
             pltpu.VMEM((moves, *chunk), F32),
@@ -360,9 +411,12 @@
             pltpu.VMEM((moves, *chunk), F32),
             pltpu.VMEM((2, n, *chunk), F32),
             pltpu.VMEM((wide, size), BF16),
-            pltpu.VMEM((depth, size), BF16),
             pltpu.VMEM((size, depth), BF16),
             pltpu.VMEM((depth, size), F32),
+            pltpu.VMEM((size, depth), BF16),
+            pltpu.VMEM((size, depth), BF16),
+            pltpu.VMEM((depth, size), BF16),
+            pltpu.VMEM((depth, size), BF16),
             pltpu.VMEM((size, size), F32),
             pltpu.VMEM((size, size), F32),
             pltpu.VMEM((2, bits + 1, size, size), F32),

time: 98.3 us -> 90 us (0.916)
  Pallas kernels: 92.5 us -> 84.2 us
    pallas_call x1, Pallas kernels: 92.5 us -> 84.2 us  [on_device(): pl.pallas_call(functools.partial(kernel, n, experts, float(depth * n * wi...]
where the time goes in v2:
time: 90 us; the launch traced here: 89.8 us
  Pallas kernels  84.2 us (94%)
  local copies, waits for them, and re-layouts  3.7 us (4%)
  between operations  1.94 us (2%)
    pallas_call x1, Pallas kernels, on_device(): pl.pallas_call(functools.partial(kernel, n, experts, float(depth * n * wi...  84.2 us
    unnamed x4, local copies, waits for them, and re-layouts  3.7 us

profile of v2, /device:TPU:0, one launch (start us, length us, event | category | flops | bytes accessed | tf_op | source)
XLA Modules:
  0.0 89.8 jit_solution(14122672194137465014)
XLA Ops:
  1.9 84.2 %shard_map.59 = (f32[1792,256]{1,0:T(8,128)}, f32[256,512]{1,0:T(8,128)}) custom-call(bf16[1792,2048]{1,0:T(8,128)(2,1)} %bitcast.4, bf16[1792,256]{1,0:T(8,128)(2,1)} %bitcast.6, s32[1]{0:T(128)S(6)} %copy.8.live_ref, s32[1]{0:T(128)S(6)} %select_n.4.refresh_ref), custom_call_target="tpu_custom_call" | custom-call | tf_op jit(solution)/shard_map/pallas_call | solution.py:396
  86.1 0.0 copy-start
  86.1 2.9 %copy.10 = f32[1,1792,256]{2,1,0:T(8,128)} copy(f32[1,1792,256]{2,1,0:T(8,128)} %bitcast.5) | data formatting | bytes 3670016
  89.0 0.0 copy-done
  89.0 0.8 copy.11
Async XLA Ops:
  86.1 2.9 %copy-start = (f32[256,512]{1,0:T(8,128)S(1)}, f32[256,512]{1,0:T(8,128)}, u32[]{:S(2)}) copy-start(f32[256,512]{1,0:T(8,128)} %get-tuple-element.5) | copy-start | bytes 1572868
